TPU v7x, 128 devices: a whole 4x4x4 slice. The times are simulated.
128 devices in a mesh: items: 32 (over y, z, core), users: 4 (over x).
Axes of the slice: x: 4, y: 4, z: 4, core: 2. Of those that a mesh axis runs over, the one named last changes fastest.
Arguments:
- user_emb: bfloat16 [4096, 256], P('users', 'items'), as said below
- item_emb: bfloat16 [1048576, 256], P('items'), as said below
- target: int32 [4096], P('users'), may hold values from 0 to 1048575
- history: int32 [4096, 32], P('users'), may hold values from 0 to 1048575, as said below
Outputs:
- log_rank: float32 [4096], P('users')
- metrics: float32 [2], replicated
Inputs may be any that keep to these rules, and one draw needn't show every extreme that they name: history[u, k] lies in [k * 32768, (k + 1) * 32768); a user's history entries are thus distinct. `item_emb`: rows of norm about one. `user_emb`: entries of order one.
All inputs are finite; a program needn't handle non-finite values.
Results may differ from a plain program's by a relative error of at most 0.0003.
Values may be sent and summed in bfloat16 or wider, within the bound.
A program may use at most 64 MiB of HBM per device.

v0:
```python
import jax
import jax.numpy as jnp
from jax import lax
from jax.sharding import PartitionSpec as P

sharpness = 4.0


def joined_along(pieces, dim):
    pieces = jnp.moveaxis(pieces, 0, dim)
    shape = pieces.shape
    return pieces.reshape(*shape[:dim], shape[dim] * shape[dim + 1], *shape[dim + 2 :])


def from_everyone(shard, axis):
    copies = jnp.broadcast_to(shard, (lax.axis_size(axis), *shard.shape))
    return lax.all_to_all(copies, axis, split_axis=0, concat_axis=0, tiled=True)


def gather_directly(shard, axis, dim):
    return joined_along(from_everyone(shard, axis), dim)


def over_copies(shard, axis):
    return from_everyone(shard, axis).sum(axis=0)


def together(arrays, axis):
    ends = [0]
    for a in arrays:
        ends.append(ends[-1] + a.size)
    so_far = over_copies(jnp.concatenate([a.ravel() for a in arrays]), axis)
    return tuple((so_far[b:e].reshape(a.shape) for a, b, e in zip(arrays, ends, ends[1:])))


def body(user_emb, item_emb, target, history):
    item_dev = item_emb.shape[0]
    shard = lax.axis_index("items")
    start = shard * item_dev
    local_t = target - start
    inside = (local_t >= 0) & (local_t < item_dev)
    own_rows = item_emb[jnp.clip(local_t, 0, item_dev - 1)]
    users = gather_directly(user_emb, "items", 1)
    partial_t = jnp.sum(users.astype(jnp.float32) * own_rows.astype(jnp.float32), axis=1)
    tscore = over_copies(jnp.where(inside, partial_t, 0.0), "items")
    n_items = lax.axis_size("items")
    n_users = lax.axis_size("users")
    u_dev = users.shape[0]
    blk = min(item_dev, 4096)
    nblk = item_dev // blk

    def add_block(index, total):
        rows = lax.dynamic_slice_in_dim(item_emb, index * blk, blk, 0)
        score = lax.dot_general(
            users, rows, (((1,), (1,)), ((), ())), preferred_element_type=jnp.float32
        )
        return total + jnp.sum(jax.nn.sigmoid(sharpness * (score - tscore[:, None])), axis=1)

    total = lax.fori_loop(0, nblk, add_block, jnp.zeros((u_dev,), jnp.float32))
    per_shard = history.shape[1] // n_items
    own_hist = lax.dynamic_slice_in_dim(history, shard * per_shard, per_shard, 1)
    hrows = item_emb[own_hist - start]
    hscore = jnp.einsum("ud,uhd->uh", users, hrows, preferred_element_type=jnp.float32)
    local = total - jnp.sum(jax.nn.sigmoid(sharpness * (hscore - tscore[:, None])), axis=1)
    seen = jnp.any(history == target[:, None], axis=1)
    correction = jnp.where(seen, 0.0, 0.5).astype(jnp.float32)
    all_users = u_dev * n_users
    above = over_copies(local, "items") - correction
    rank = 1.0 + above
    log_rank = jnp.log(rank)
    hit = jax.nn.sigmoid(10.5 - rank)
    gain = hit / jnp.log2(1.0 + rank)
    hit_sum, gain_sum = together((jnp.sum(hit), jnp.sum(gain)), "users")
    metrics = jnp.stack([hit_sum, gain_sum]) / all_users
    return (log_rank, metrics)


def solution(mesh):
    return jax.shard_map(
        body,
        mesh=mesh,
        in_specs=(P("users", "items"), P("items", None), P("users"), P("users", None)),
        out_specs=(P("users"), P()),
        check_vma=False,
    )
```

profile of v0, /device:TPU:0, one launch (start us, length us, event | category | flops | bytes accessed | tf_op | source)
XLA Modules:
  0.0 130.2 jit_solution(8340688998391496032)
XLA Ops:
  0.6 1.6 %broadcast_in_dim.35 = bf16[32,1024,8]{1,2,0:T(8,128)(2,1)} broadcast(bf16[1024,8]{0,1:T(8,128)(2,1)} %param.6), dimensions={1,2} | broadcast | bytes 540672 | tf_op jit(solution)/shard_map/broadcast_in_dim | solution.py:16
  2.2 8.4 %all-to-all-start = ((bf16[32,1024,8]{1,2,0:T(8,128)(2,1)}), bf16[32,1024,8]{1,2,0:T(8,128)(2,1)S(1)}, u32[]{:S(2)}, u32[]{:S(2)}) async-start(bf16[32,1024,8]{1,2,0:T(8,128)(2,1)} %broadcast_in_dim.35), calls=%async_computation | async-start | bytes 1048576 | tf_op jit(solution)/shard_map/all_to_all | solution.py:17
  10.7 0.8 compare_select_fusion
  11.5 11.4 %gather_fusion.1 = bf16[1024,256]{1,0:T(8,128)(2,1)S(1)} fusion(bf16[32768,256]{1,0:T(8,128)(2,1)} %param.7, s32[1024]{0:T(1024)S(1)} %broadcast_clamp_fusion), kind=kCustom, calls=%fused_computation.1 | custom fusion | bytes 1052672 | tf_op jit(solution)/shard_map/gather | solution.py:62
  22.8 0.2 copy.19
  23.1 0.7 fusion.4
  23.8 11.4 %gather_fusion = bf16[1024,256]{1,0:T(8,128)(2,1)S(1)} fusion(bf16[32768,256]{1,0:T(8,128)(2,1)} %param.7, s32[1024]{0:T(1024)S(1)} %fusion.4), kind=kCustom, calls=%fused_computation | custom fusion | bytes 1052672 | tf_op jit(solution)/shard_map/gather | solution.py:42
  35.2 0.2 copy.11
  35.4 0.0 all-to-all-done
  35.4 0.2 fusion.3
  35.5 0.7 and_select_fusion
  36.2 0.7 broadcast_in_dim.37
  36.9 7.4 %all-to-all-start.1 = ((f32[32,1,1024]{2,1,0:T(1,128)}), f32[32,1,1024]{2,1,0:T(1,128)S(1)}, u32[]{:S(2)}, u32[]{:S(2)}) async-start(f32[32,1,1024]{2,1,0:T(1,128)} %broadcast_in_dim.37), calls=%async_computation.1 | async-start | bytes 262144 | tf_op jit(solution)/shard_map/all_to_all | solution.py:17
  44.3 0.2 copy.13
  44.5 0.2 multiply_reduce_fusion
  44.7 7.5 %all-to-all-done.1 = f32[32,1,1024]{2,1,0:T(1,128)S(1)} async-done(((f32[32,1,1024]{2,1,0:T(1,128)}), f32[32,1,1024]{2,1,0:T(1,128)S(1)}, u32[]{:S(2)}, u32[]{:S(2)}) %all-to-all-start.1) | async-done | bytes 131104 | tf_op jit(solution)/shard_map/all_to_all | solution.py:17
  52.2 0.1 reduce_sum.72
  52.3 0.0 copy-start
  52.3 0.0 copy-start.1
  52.3 52.8 %while.14 = (s32[]{:T(128)}, f32[1024]{0:T(1024)S(1)}, bf16[32768,256]{1,0:T(8,128)(2,1)}, bf16[1024,256]{1,0:T(8,128)(2,1)S(1)}, f32[1024]{0:T(1024)S(1)}, /*index=5*/s32[]{:T(128)}, s32[]{:T(128)}, s32[]{:T(128)}, s32[]{:T(128)}) while((s32[]{:T(128)}, f32[1024]{0:T(1024)S(1)}, bf16[32768,256]{1,0:T(8,128)(2,1)}, ...), condition=%wide.region_4.5_spmd.clone, body=%wide.region_2.4_spmd.clone.sunk | while | flops 2172650496 | bytes 2642073 | solution.py:59
  52.3 6.6 %fusion.11 = f32[1024]{0:T(1024)S(1)} fusion(bf16[1024,256]{1,0:T(8,128)(2,1)S(1)} %get-tuple-element.195, f32[1024]{0:T(1024)S(1)} %get-tuple-element.196, bf16[32768,256]{1,0:T(8,128)(2,1)} %get-tuple-element.194, s32[]{:T(128)S(6)} %select_n.43), kind=kOutput, calls=%fused_computation.3.clone.1 | convolution fusion | flops 2172648448 | bytes 2629636 | tf_op jit(solution)/shard_map/while/body/eval_jaxpr/dot_general | solution.py:54
  58.9 6.5 %fusion.11 = f32[1024]{0:T(1024)S(1)} fusion(bf16[1024,256]{1,0:T(8,128)(2,1)S(1)} %get-tuple-element.195, f32[1024]{0:T(1024)S(1)} %get-tuple-element.196, bf16[32768,256]{1,0:T(8,128)(2,1)} %get-tuple-element.194, s32[]{:T(128)S(6)} %select_n.43), kind=kOutput, calls=%fused_computation.3.clone.1 | convolution fusion | flops 2172648448 | bytes 2629636 | tf_op jit(solution)/shard_map/while/body/eval_jaxpr/dot_general | solution.py:54
  65.5 6.5 %fusion.11 = f32[1024]{0:T(1024)S(1)} fusion(bf16[1024,256]{1,0:T(8,128)(2,1)S(1)} %get-tuple-element.195, f32[1024]{0:T(1024)S(1)} %get-tuple-element.196, bf16[32768,256]{1,0:T(8,128)(2,1)} %get-tuple-element.194, s32[]{:T(128)S(6)} %select_n.43), kind=kOutput, calls=%fused_computation.3.clone.1 | convolution fusion | flops 2172648448 | bytes 2629636 | tf_op jit(solution)/shard_map/while/body/eval_jaxpr/dot_general | solution.py:54
  72.1 6.5 %fusion.11 = f32[1024]{0:T(1024)S(1)} fusion(bf16[1024,256]{1,0:T(8,128)(2,1)S(1)} %get-tuple-element.195, f32[1024]{0:T(1024)S(1)} %get-tuple-element.196, bf16[32768,256]{1,0:T(8,128)(2,1)} %get-tuple-element.194, s32[]{:T(128)S(6)} %select_n.43), kind=kOutput, calls=%fused_computation.3.clone.1 | convolution fusion | flops 2172648448 | bytes 2629636 | tf_op jit(solution)/shard_map/while/body/eval_jaxpr/dot_general | solution.py:54
  78.7 6.5 %fusion.11 = f32[1024]{0:T(1024)S(1)} fusion(bf16[1024,256]{1,0:T(8,128)(2,1)S(1)} %get-tuple-element.195, f32[1024]{0:T(1024)S(1)} %get-tuple-element.196, bf16[32768,256]{1,0:T(8,128)(2,1)} %get-tuple-element.194, s32[]{:T(128)S(6)} %select_n.43), kind=kOutput, calls=%fused_computation.3.clone.1 | convolution fusion | flops 2172648448 | bytes 2629636 | tf_op jit(solution)/shard_map/while/body/eval_jaxpr/dot_general | solution.py:54
  85.3 6.5 %fusion.11 = f32[1024]{0:T(1024)S(1)} fusion(bf16[1024,256]{1,0:T(8,128)(2,1)S(1)} %get-tuple-element.195, f32[1024]{0:T(1024)S(1)} %get-tuple-element.196, bf16[32768,256]{1,0:T(8,128)(2,1)} %get-tuple-element.194, s32[]{:T(128)S(6)} %select_n.43), kind=kOutput, calls=%fused_computation.3.clone.1 | convolution fusion | flops 2172648448 | bytes 2629636 | tf_op jit(solution)/shard_map/while/body/eval_jaxpr/dot_general | solution.py:54
  91.9 6.5 %fusion.11 = f32[1024]{0:T(1024)S(1)} fusion(bf16[1024,256]{1,0:T(8,128)(2,1)S(1)} %get-tuple-element.195, f32[1024]{0:T(1024)S(1)} %get-tuple-element.196, bf16[32768,256]{1,0:T(8,128)(2,1)} %get-tuple-element.194, s32[]{:T(128)S(6)} %select_n.43), kind=kOutput, calls=%fused_computation.3.clone.1 | convolution fusion | flops 2172648448 | bytes 2629636 | tf_op jit(solution)/shard_map/while/body/eval_jaxpr/dot_general | solution.py:54
  98.5 6.5 %fusion.11 = f32[1024]{0:T(1024)S(1)} fusion(bf16[1024,256]{1,0:T(8,128)(2,1)S(1)} %get-tuple-element.195, f32[1024]{0:T(1024)S(1)} %get-tuple-element.196, bf16[32768,256]{1,0:T(8,128)(2,1)} %get-tuple-element.194, s32[]{:T(128)S(6)} %select_n.43), kind=kOutput, calls=%fused_computation.3.clone.1 | convolution fusion | flops 2172648448 | bytes 2629636 | tf_op jit(solution)/shard_map/while/body/eval_jaxpr/dot_general | solution.py:54
  105.1 0.7 broadcast_in_dim.39
  105.8 3.9 %all-to-all-start.2 = ((f32[32,1,1024]{2,1,0:T(1,128)}), f32[32,1,1024]{2,1,0:T(1,128)S(1)}, u32[]{:S(2)}, u32[]{:S(2)}) async-start(f32[32,1,1024]{2,1,0:T(1,128)} %broadcast_in_dim.39), calls=%async_computation.2 | async-start | bytes 262144 | tf_op jit(solution)/shard_map/all_to_all | solution.py:17
  109.6 0.0 copy-done
  109.6 0.0 copy-done.1
  109.7 7.8 %all-to-all-done.2 = f32[32,1,1024]{2,1,0:T(1,128)S(1)} async-done(((f32[32,1,1024]{2,1,0:T(1,128)}), f32[32,1,1024]{2,1,0:T(1,128)S(1)}, u32[]{:S(2)}, u32[]{:S(2)}) %all-to-all-start.2) | async-done | bytes 131104 | tf_op jit(solution)/shard_map/all_to_all | solution.py:17
  117.5 0.1 reduce_sum.73
  117.6 1.3 divide_reduce_fusion.1
  118.8 1.4 %pad_maximum_fusion = f32[2]{0:T(128)S(1)} fusion(f32[1]{0:T(128)} %bitcast.6, f32[1]{0:T(128)} %bitcast.5), kind=kLoop, calls=%fused_computation.22 | loop fusion | flops 2 | bytes 16 | tf_op jit(solution)/shard_map/concatenate | solution.py:32
  120.3 9.4 %all_to_all.23 = f32[4,1,2]{2,1,0:T(1,128)S(1)} all-to-all(f32[4,1,2]{2,1,0:T(1,128)S(1)} %broadcast_in_dim.41), channel_id=1, replica_groups=mesh['items'=32,'users'=4] {'users'}, dimensions={0} | all-to-all | bytes 64 | tf_op jit(solution)/shard_map/all_to_all | solution.py:17
  129.7 0.5 broadcast_multiply_fusion
  (14 shorter events, 0.1 us)
Async XLA Ops:
  2.2 33.2 %all-to-all-start = ((bf16[32,1024,8]{1,2,0:T(8,128)(2,1)}), bf16[32,1024,8]{1,2,0:T(8,128)(2,1)S(1)}, u32[]{:S(2)}, u32[]{:S(2)}) async-start(bf16[32,1024,8]{1,2,0:T(8,128)(2,1)} %broadcast_in_dim.35), calls=%async_computation | async-start | bytes 1048576 | tf_op jit(solution)/shard_map/all_to_all | solution.py:17
  36.9 15.2 %all-to-all-start.1 = ((f32[32,1,1024]{2,1,0:T(1,128)}), f32[32,1,1024]{2,1,0:T(1,128)S(1)}, u32[]{:S(2)}, u32[]{:S(2)}) async-start(f32[32,1,1024]{2,1,0:T(1,128)} %broadcast_in_dim.37), calls=%async_computation.1 | async-start | bytes 262144 | tf_op jit(solution)/shard_map/all_to_all | solution.py:17
  52.3 57.4 %copy-start = (s32[1024,32]{0,1:T(8,128)S(1)}, s32[1024,32]{0,1:T(8,128)}, u32[]{:S(2)}) copy-start(s32[1024,32]{0,1:T(8,128)} %param.9) | copy-start | bytes 393220
  52.3 57.4 %copy-start.1 = (s32[1024]{0:T(1024)S(1)}, s32[1024]{0:T(1024)}, u32[]{:S(2)}) copy-start(s32[1024]{0:T(1024)} %param.8) | copy-start | bytes 12292
  105.8 11.7 %all-to-all-start.2 = ((f32[32,1,1024]{2,1,0:T(1,128)}), f32[32,1,1024]{2,1,0:T(1,128)S(1)}, u32[]{:S(2)}, u32[]{:S(2)}) async-start(f32[32,1,1024]{2,1,0:T(1,128)} %broadcast_in_dim.39), calls=%async_computation.2 | async-start | bytes 262144 | tf_op jit(solution)/shard_map/all_to_all | solution.py:17
where the time goes:
time: 131 us; the launch traced here: 130 us
  matrix products  52.4 us (40%)
  local copies, waits for them, and re-layouts  26.4 us (20%)
  starting transfers between devices  19.7 us (15%)
  waiting for transfers between devices  15.3 us (12%)
  blocking collectives  9.37 us (7%)
  other arithmetic  6 us (5%)
    dot_general x8, matrix products, add_block(): lax.dot_general(users, rows, (((1,), (1,)), ((), ())), preferred_element_...  52.4 us
    all_to_all x3, starting transfers between devices, from_everyone(): return lax.all_to_all(copies, axis, split_axis=0, concat_axis=0, tiled=True)  19.7 us
    all_to_all x3, waiting for transfers between devices, from_everyone(): return lax.all_to_all(copies, axis, split_axis=0, concat_axis=0, tiled=True)  15.3 us
    gather x1, local copies, waits for them, and re-layouts, body(): hrows = item_emb[own_hist - start]  11.4 us
    gather x1, local copies, waits for them, and re-layouts, body(): own_rows = item_emb[jnp.clip(local_t, 0, item_dev - 1)]  11.4 us
    all_to_all x1, blocking collectives, from_everyone(): return lax.all_to_all(copies, axis, split_axis=0, concat_axis=0, tiled=True)  9.37 us
    broadcast_in_dim x4, local copies, waits for them, and re-layouts, from_everyone(): copies = jnp.broadcast_to(shard, (lax.axis_size(axis), *shard.shape))  2.99 us
  transfers between devices with their start and end apart: 3, of which 2 were waited for; matrix products, arithmetic and copies ran while one was open for 19% of the time, Pallas kernels for 0%

commit v1 on v0

v1 whole, which is shorter than its diff:
```python
import functools

import jax
import jax.numpy as jnp
from jax import lax
from jax.experimental import pallas as pl
from jax.experimental.pallas import tpu as pltpu
from jax.sharding import PartitionSpec as P

MESH = pl.DeviceIdType.MESH
SHARP_HALF = 2.0
ROWS = 2048
PARTS = 8


def to_peers(src, dst, send, recv, axis, me, n):
    for j in range(1, n):
        pltpu.make_async_remote_copy(
            src_ref=src, dst_ref=dst.at[me], send_sem=send, recv_sem=recv,
            device_id={axis: lax.rem(me + j, n)}, device_id_type=MESH,
        ).start()


def wait_bytes(ref, send, recv, axis):
    d = pltpu.make_async_remote_copy(
        src_ref=ref, dst_ref=ref, send_sem=send, recv_sem=recv,
        device_id={axis: 0}, device_id_type=MESH,
    )
    d.wait_recv()
    d.wait_send()


def kernel(ni, nu, u_ref, t_ref, h_ref, ts_ref, hh_ref, items_ref, out_ref, met_ref,
           buf, uall, U, gt, gh, hs, tval, lval, mval, trecv, lrecv, mrecv,
           isem, hsem, us, ur, ps, pr, tsd, trc, lsd, lrc, msd, mrc):
    n_tiles, sub, d = buf.shape
    n_rows = n_tiles * sub
    users = t_ref.shape[1]
    tiles = users // 256
    me = lax.axis_index("items")
    mx = lax.axis_index("users")
    core = lax.rem(me, 2)
    chip = me // 2
    chips = ni // 2
    partner = chip * 2 + 1 - core
    start = me * n_rows

    part = n_tiles // PARTS
    copies = [
        pltpu.make_async_copy(items_ref.at[pl.ds(p * part, part)], buf.at[pl.ds(p * part, part)], isem.at[p])
        for p in range(PARTS)
    ]
    hcopy = pltpu.make_async_copy(hh_ref.at[pl.ds(pl.multiple_of((me // 8) * 8, 8), 8)], hs, hsem)
    hcopy.start()
    for c in copies:
        c.start()

    barrier = pltpu.get_barrier_semaphore()
    for j in range(1, ni):
        pl.semaphore_signal(barrier, inc=1, device_id={"items": lax.rem(me + j, ni)}, device_id_type=MESH)
    for j in range(1, nu):
        pl.semaphore_signal(barrier, inc=1, device_id={"users": lax.rem(mx + j, nu)}, device_id_type=MESH)
    pl.semaphore_wait(barrier, ni + nu - 2)

    for j in range(1, chips):
        pltpu.make_async_remote_copy(
            src_ref=u_ref, dst_ref=uall.at[me], send_sem=us, recv_sem=ur,
            device_id={"items": lax.rem(chip + j, chips) * 2 + core}, device_id_type=MESH,
        ).start()
    uall[me] = u_ref[...]

    row16 = lax.broadcasted_iota(jnp.int32, (16, 128), 0)
    lane16 = lax.broadcasted_iota(jnp.int32, (16, 256), 1)

    def pick(index, rows_ref):
        def step(i, carry):
            for c in range(4):
                base = i * 64 + c * 16
                picked = []
                place = jnp.zeros((16, 128), jnp.int32)
                for j in range(16):
                    row = index(base + j)
                    tile = lax.shift_right_logical(row, 4)
                    picked.append(buf[tile])
                    place = jnp.where(row16 == j, (row & 15) + 16 * j, place)
                place = jnp.concatenate([place, place], axis=1)
                onehot = (place == lane16).astype(jnp.float32).astype(jnp.bfloat16)
                rows = jnp.dot(onehot, jnp.concatenate(picked, axis=0), preferred_element_type=jnp.float32)
                rows_ref[pl.ds(pl.multiple_of(base, 16), 16), :] = rows.astype(jnp.bfloat16)
            return carry
        lax.fori_loop(0, users // 64, step, 0)

    hcopy.wait()
    for c in copies:
        c.wait()
    pick(lambda k: jnp.minimum(jnp.maximum(ts_ref[k] - start, 0), n_rows - 1), gt)

    wait_bytes(uall.at[pl.ds(0, chips - 1)], us, ur, "items")
    for j in range(chips):
        k = lax.rem(chip + j, chips) * 2 + core
        pltpu.make_async_remote_copy(
            src_ref=uall.at[k], dst_ref=uall.at[k], send_sem=ps, recv_sem=pr,
            device_id={"items": partner}, device_id_type=MESH,
        ).start()
    hrow = lax.rem(me, 8)
    pick(lambda k: jnp.minimum(jnp.maximum(hs[hrow, k] - start, 0), n_rows - 1), gh)
    wait_bytes(uall.at[pl.ds(0, chips)], ps, pr, "items")

    for k in range(d // 16):
        two = jnp.concatenate([uall[2 * k].astype(jnp.float32), uall[2 * k + 1].astype(jnp.float32)], axis=0)
        U[16 * k:16 * k + 16, :] = (two * SHARP_HALF).astype(jnp.bfloat16)

    eye = lax.broadcasted_iota(jnp.int32, (256, 256), 0) == lax.broadcasted_iota(jnp.int32, (256, 256), 1)

    def own_scores(rows_ref):
        out = []
        for q in range(tiles):
            s = jnp.dot(rows_ref[q * 256:(q + 1) * 256, :], U[:, q * 256:(q + 1) * 256],
                        preferred_element_type=jnp.float32)
            out.append(jnp.sum(jnp.where(eye, s, 0.0), axis=0, keepdims=True))
        return jnp.concatenate(out, axis=1)

    local_t = t_ref[...] - start
    inside = (local_t >= 0) & (local_t < n_rows)
    mine = jnp.where(inside, own_scores(gt), 0.0)
    tval[...] = mine
    to_peers(tval, trecv, tsd, trc, "items", me, ni)
    trecv[me] = mine
    hscore = own_scores(gh)
    wait_bytes(trecv.at[pl.ds(0, ni - 1)], tsd, trc, "items")
    tscore = trecv[0]
    for k in range(1, ni):
        tscore = tscore + trecv[k]

    def block(i, sums):
        rows = buf[pl.ds(i * (ROWS // sub), ROWS // sub)].reshape(ROWS, d)
        out = []
        for q in range(tiles):
            s = jnp.dot(rows, U[:, q * 256:(q + 1) * 256], preferred_element_type=jnp.float32)
            y = jnp.tanh(s - tscore[:, q * 256:(q + 1) * 256]) + 1.0
            out.append(sums[q] + jnp.sum(y.reshape(ROWS // 8, 8, 256), axis=0))
        return tuple(out)

    zero = jnp.zeros((8, 256), jnp.float32)
    sums = lax.fori_loop(0, n_rows // ROWS, block, (zero,) * tiles)
    total = jnp.concatenate([jnp.sum(s, axis=0, keepdims=True) for s in sums], axis=1)
    local = 0.5 * (total - (jnp.tanh(hscore - tscore) + 1.0))
    lval[...] = local
    to_peers(lval, lrecv, lsd, lrc, "items", me, ni)
    lrecv[me] = local
    seen = jnp.max(jnp.where(h_ref[...] == t_ref[...], 1.0, 0.0), axis=0, keepdims=True)
    correction = 0.5 - 0.5 * seen
    wait_bytes(lrecv.at[pl.ds(0, ni - 1)], lsd, lrc, "items")
    count = lrecv[0]
    for k in range(1, ni):
        count = count + lrecv[k]
    rank = 1.0 + (count - correction)
    out_ref[...] = jnp.log(rank)
    hit = 1.0 / (1.0 + jnp.exp(rank - 10.5))
    gain = hit * (0.6931471805599453 / jnp.log(1.0 + rank))

    def lanes(v):
        acc = v[:, 0:128]
        for g in range(1, users // 128):
            acc = acc + v[:, g * 128:(g + 1) * 128]
        return acc

    both = jnp.concatenate([lanes(hit), lanes(gain)], axis=0)
    mval[...] = both
    to_peers(mval, mrecv, msd, mrc, "users", mx, nu)
    mrecv[mx] = both
    wait_bytes(mrecv.at[pl.ds(0, nu - 1)], msd, mrc, "users")
    met = mrecv[0]
    for k in range(1, nu):
        met = met + mrecv[k]
    met_ref[...] = jnp.sum(met, axis=1, keepdims=True) * (1.0 / (users * nu))


def body(user_emb, item_emb, target, history):
    ni = lax.axis_size("items")
    nu = lax.axis_size("users")
    users = target.shape[0]
    n_rows, d = item_emb.shape
    vmem = pl.BlockSpec(memory_space=pltpu.VMEM)
    hbm = pl.BlockSpec(memory_space=pl.ANY)
    dma = pltpu.SemaphoreType.DMA
    ht = history.T
    lr, met = pl.pallas_call(
        functools.partial(kernel, ni, nu),
        out_shape=(jax.ShapeDtypeStruct((1, users), jnp.float32), jax.ShapeDtypeStruct((2, 1), jnp.float32)),
        in_specs=[vmem, vmem, vmem, pl.BlockSpec(memory_space=pltpu.SMEM), hbm, hbm],
        out_specs=(vmem, vmem),
        scratch_shapes=[
            pltpu.VMEM((n_rows // 16, 16, d), jnp.bfloat16),
            pltpu.VMEM((ni, d // ni, users), jnp.bfloat16),
            pltpu.VMEM((d, users), jnp.bfloat16),
            pltpu.VMEM((users, d), jnp.bfloat16),
            pltpu.VMEM((users, d), jnp.bfloat16),
            pltpu.SMEM((8, users), jnp.int32),
            pltpu.VMEM((1, users), jnp.float32),
            pltpu.VMEM((1, users), jnp.float32),
            pltpu.VMEM((2, 128), jnp.float32),
            pltpu.VMEM((ni, 1, users), jnp.float32),
            pltpu.VMEM((ni, 1, users), jnp.float32),
            pltpu.VMEM((nu, 2, 128), jnp.float32),
            dma((PARTS,)), dma, dma, dma, dma, dma, dma, dma, dma, dma, dma, dma,
        ],
        compiler_params=pltpu.CompilerParams(
            collective_id=0, has_side_effects=True, vmem_limit_bytes=56 * 2**20
        ),
        name="rank_metrics",
    )(user_emb.T, target.reshape(1, users), ht, target, ht, item_emb.reshape(n_rows // 16, 16, d))
    return lr.reshape(users), met.reshape(2)


def solution(mesh):
    return jax.shard_map(
        body,
        mesh=mesh,
        in_specs=(P("users", "items"), P("items", None), P("users"), P("users", None)),
        out_specs=(P("users"), P()),
        check_vma=False,
    )
```

time: 131 us -> 61.6 us (0.47)
  Pallas kernels: 0 us -> 58.2 us
  matrix products: 52.4 us -> 0 us
  local copies, waits for them, and re-layouts: 26.4 us -> 1.27 us
  starting transfers between devices: 19.7 us -> 0 us
  waiting for transfers between devices: 15.3 us -> 0 us
  blocking collectives: 9.37 us -> 0 us
  other arithmetic: 6 us -> 1.29 us
    pallas_call x0 -> x1, Pallas kernels: none -> 58.2 us  [body(): pl.pallas_call(functools.partial(kernel, ni, nu), out_shape=(jax.ShapeDty...]
    dot_general x8 -> x0, matrix products: 52.4 us -> none  [add_block(): lax.dot_general(users, rows, (((1,), (1,)), ((), ())), preferred_element_...]
    gather x2 -> x0, local copies, waits for them, and re-layouts: 22.8 us -> none  [the longest x1 11.4 us: body(): hrows = item_emb[own_hist - start]]
    all_to_all x3 -> x0, starting transfers between devices: 19.7 us -> none  [from_everyone(): return lax.all_to_all(copies, axis, split_axis=0, concat_axis=0, tiled=True)]
    all_to_all x3 -> x0, waiting for transfers between devices: 15.3 us -> none  [from_everyone(): return lax.all_to_all(copies, axis, split_axis=0, concat_axis=0, tiled=True)]
    all_to_all x1 -> x0, blocking collectives: 9.37 us -> none  [from_everyone(): return lax.all_to_all(copies, axis, split_axis=0, concat_axis=0, tiled=True)]
    broadcast_in_dim x4 -> x0, local copies, waits for them, and re-layouts: 2.99 us -> none  [from_everyone(): copies = jnp.broadcast_to(shard, (lax.axis_size(axis), *shard.shape))]
    reduce_sum x5 -> x0, other arithmetic: 1.66 us -> none  [the longest x1 1.29 us: body(): hit_sum, gain_sum = together((jnp.sum(hit), jnp.sum(gain)), 'users')]
  transfers between devices with their start and end apart: 3 -> 0, of which waited for: 2 -> 0; matrix products, arithmetic and copies ran while one was open for 19% -> 0% of each run, Pallas kernels for 0% -> 0%
where the time goes in v1:
time: 61.6 us; the launch traced here: 61.4 us
  Pallas kernels  58.2 us (94%)
  other arithmetic  1.29 us (2%)
  local copies, waits for them, and re-layouts  1.27 us (2%)
  between operations  0.64 us (1%)
    pallas_call x1, Pallas kernels, body(): pl.pallas_call(functools.partial(kernel, ni, nu), out_shape=(jax.ShapeDty...  58.2 us
    pallas_call x1, other arithmetic, body(): pl.pallas_call(functools.partial(kernel, ni, nu), out_shape=(jax.ShapeDty...  1.29 us
    unnamed x1, local copies, waits for them, and re-layouts  1.27 us

profile of v1, /device:TPU:0, one launch (start us, length us, event | category | flops | bytes accessed | tf_op | source)
XLA Modules:
  0.0 61.4 jit_solution(3771040275711914403)
XLA Ops:
  0.6 58.2 %rank_metrics.1 = (f32[1,1024]{1,0:T(1,128)}, f32[2,1]{1,0:T(2,128)}) custom-call(bf16[8,1024]{1,0:T(8,128)(2,1)} %bitcast.8, s32[1,1024]{1,0:T(1,128)} %bitcast.9, s32[32,1024]{1,0:T(8,128)} %bitcast.6, s32[1024]{0:T(1024)} %ts_ref.1, s32[32,1024]{1,0:T(8,128)} %bitcast.7, bf16[2048,16,256]{2,1,0:T(8,128)(2,1)} %bitcast.5), custom_call_target="tpu_custom_call" | custom-call | tf_op jit(solution)/shard_map/rank_metrics/pallas_call | solution.py:188
  58.8 1.3 %reduce = f32[2]{0:T(128)} reduce(f32[2,1]{1,0:T(2,128)} %get-tuple-element.5, f32[]{:T(128)} %constant.1), dimensions={1}, to_apply=%get-tuple-element.5.reduce_sub_computation | reduce | bytes 20 | tf_op jit(solution)/shard_map/rank_metrics/pallas_call | solution.py:188
  60.1 1.3 %copy.7 = f32[1024]{0:T(1024)} copy(f32[1024]{0:T(1024)} %bitcast.10) | data formatting | bytes 8192

commit v2 on v1

v2 whole, which is shorter than its diff:
```python
import functools

import jax
import jax.numpy as jnp
from jax import lax
from jax.experimental import pallas as pl
from jax.experimental.pallas import tpu as pltpu
from jax.sharding import PartitionSpec as P

MESH = pl.DeviceIdType.MESH
SHARP_HALF = 2.0
ROWS = 8192
PARTS = 8


HALVES = 2


def by_distance(sides):
    steps = [()]
    for n in sides:
        steps = [s + (k,) for s in steps for k in range(n)]
    far = lambda s: sum(min(k, n - k) for k, n in zip(s, sides))
    return sorted((s for s in steps if any(s)), key=far, reverse=True)


def wait_bytes(ref, send, recv, axis):
    d = pltpu.make_async_remote_copy(
        src_ref=ref, dst_ref=ref, send_sem=send, recv_sem=recv,
        device_id={axis: 0}, device_id_type=MESH,
    )
    d.wait_recv()
    d.wait_send()


def kernel(ni, nu, u_ref, t_ref, h_ref, items_ref, out_ref, met_ref,
           buf, uall, U, gt, gh, where_v, where_s, tval, lval, mval, trecv, lrecv, mrecv,
           isem, wsem, us, ur, ps, pr, tsd, trc, lsd, lrc, msd, mrc):
    n_tiles, sub, d = buf.shape
    n_rows = n_tiles * sub
    users = t_ref.shape[1]
    half = users // HALVES
    tiles = half // 256
    me = lax.axis_index("items")
    mx = lax.axis_index("users")
    core = lax.rem(me, 2)
    chip = me // 2
    chips = ni // 2
    side = 4
    z = lax.rem(chip, side)
    y = chip // side
    partner = chip * 2 + 1 - core
    start = me * n_rows

    def peer(step):
        return (lax.rem(y + step[0], side) * side + lax.rem(z + step[1], side)) * 2 + lax.rem(core + step[2], 2)

    everyone = by_distance((ni // (2 * side), side, 2))
    same_core = [s for s in everyone if s[2] == 0]

    def to_all(src, dst, send, recv, steps):
        for s in steps:
            pltpu.make_async_remote_copy(
                src_ref=src, dst_ref=dst, send_sem=send, recv_sem=recv,
                device_id={"items": peer(s)}, device_id_type=MESH,
            ).start()

    part = n_tiles // PARTS
    copies = [
        pltpu.make_async_copy(items_ref.at[pl.ds(p * part, part)], buf.at[pl.ds(p * part, part)], isem.at[p])
        for p in range(PARTS)
    ]
    for c in copies:
        c.start()
    for k, ids in enumerate((t_ref[...], h_ref[pl.ds(me, 1), :])):
        slab, row = lax.shift_right_logical(ids, 4) & (n_tiles - 1), ids & (sub - 1)
        for g in range(users // 128):
            where_v[2 * k, g:g + 1, :] = slab[:, g * 128:(g + 1) * 128]
            where_v[2 * k + 1, g:g + 1, :] = row[:, g * 128:(g + 1) * 128]
    wcopy = pltpu.make_async_copy(where_v, where_s, wsem)

    barrier = pltpu.get_barrier_semaphore()
    for s in everyone:
        pl.semaphore_signal(barrier, inc=1, device_id={"items": peer(s)}, device_id_type=MESH)
    for j in range(1, nu):
        pl.semaphore_signal(barrier, inc=1, device_id={"users": lax.rem(mx + j, nu)}, device_id_type=MESH)
    wcopy.start()
    seen = jnp.max(jnp.where(h_ref[...] == t_ref[...], 1.0, 0.0), axis=0, keepdims=True)
    correction = 0.5 - 0.5 * seen
    pl.semaphore_wait(barrier, ni + nu - 2)

    for h in range(HALVES):
        to_all(u_ref.at[:, pl.ds(h * half, half)], uall.at[h, me], us.at[h], ur.at[h], same_core)
    for h in range(HALVES):
        uall[h, me] = u_ref[:, h * half:(h + 1) * half]

    row16 = lax.broadcasted_iota(jnp.int32, (16, 128), 0)
    lane16 = lax.broadcasted_iota(jnp.int32, (16, 256), 1) - 16 * lax.broadcasted_iota(jnp.int32, (16, 256), 0)
    chunks = 8

    def pick(which, rows_ref):
        def step(i, carry):
            for c in range(chunks):
                base = i * (16 * chunks) + c * 16
                picked = []
                place = jnp.zeros((16, 128), jnp.int32)
                for j in range(16):
                    picked.append(buf[where_s[2 * which, i, c * 16 + j]])
                    place = jnp.where(row16 == j, where_s[2 * which + 1, i, c * 16 + j], place)
                place = jnp.concatenate([place, place], axis=1)
                onehot = (place == lane16).astype(jnp.float32).astype(jnp.bfloat16)
                rows = jnp.dot(onehot, jnp.concatenate(picked, axis=0), preferred_element_type=jnp.float32)
                rows_ref[pl.ds(pl.multiple_of(base, 16), 16), :] = rows.astype(jnp.bfloat16)
            return carry
        lax.fori_loop(0, users // (16 * chunks), step, 0)

    def forward(h):
        wait_bytes(uall.at[h, pl.ds(0, chips - 1)], us.at[h], ur.at[h], "items")
        for s in same_core + [(0, 0, 0)]:
            k = peer(s)
            pltpu.make_async_remote_copy(
                src_ref=uall.at[h, k], dst_ref=uall.at[h, k], send_sem=ps.at[h], recv_sem=pr.at[h],
                device_id={"items": partner}, device_id_type=MESH,
            ).start()

    def join(h):
        wait_bytes(uall.at[h, pl.ds(0, chips)], ps.at[h], pr.at[h], "items")
        for k in range(d // 16):
            two = jnp.concatenate([uall[h, 2 * k].astype(jnp.float32), uall[h, 2 * k + 1].astype(jnp.float32)], axis=0)
            U[16 * k:16 * k + 16, h * half:(h + 1) * half] = (two * SHARP_HALF).astype(jnp.bfloat16)

    eye = lax.broadcasted_iota(jnp.int32, (256, 256), 0) == lax.broadcasted_iota(jnp.int32, (256, 256), 1)

    def own_scores(rows_ref, h):
        out = []
        for q in range(tiles * h, tiles * (h + 1)):
            s = jnp.dot(rows_ref[q * 256:(q + 1) * 256, :], U[:, q * 256:(q + 1) * 256],
                        preferred_element_type=jnp.float32)
            out.append(jnp.sum(jnp.where(eye, s, 0.0), axis=0, keepdims=True))
        return jnp.concatenate(out, axis=1)

    local_t = t_ref[...] - start
    inside = (local_t >= 0) & (local_t < n_rows)

    def send_tscore(h):
        mine = jnp.where(inside[:, h * half:(h + 1) * half], own_scores(gt, h), 0.0)
        tval[h] = mine
        to_all(tval.at[h], trecv.at[h, me], tsd.at[h], trc.at[h], everyone)
        trecv[h, me] = mine

    def total_of(recv, h, send_sem, recv_sem):
        wait_bytes(recv.at[h, pl.ds(0, ni - 1)], send_sem.at[h], recv_sem.at[h], "items")
        v = recv[h, 0]
        for k in range(1, ni):
            v = v + recv[h, k]
        return v

    def score(h, tscore, lo, hi, sums):
        def block(i, sums):
            rows = buf[pl.ds(i * (ROWS // sub), ROWS // sub)].reshape(ROWS, d)
            out = []
            for q in range(tiles):
                s = jnp.dot(rows, U[:, h * half + q * 256:h * half + (q + 1) * 256], preferred_element_type=jnp.float32)
                y = jnp.tanh(s - tscore[:, q * 256:(q + 1) * 256]) + 1.0
                out.append(sums[q] + jnp.sum(y.reshape(ROWS // 8, 8, 256), axis=0))
            return tuple(out)
        return lax.fori_loop(lo, hi, block, sums)

    def send_count(h, sums, hscore, tscore):
        total = jnp.concatenate([jnp.sum(s, axis=0, keepdims=True) for s in sums], axis=1)
        local = 0.5 * (total - (jnp.tanh(hscore - tscore) + 1.0))
        lval[h] = local
        to_all(lval.at[h], lrecv.at[h, me], lsd.at[h], lrc.at[h], everyone)
        lrecv[h, me] = local

    def lanes(v):
        acc = v[:, 0:128]
        for g in range(1, half // 128):
            acc = acc + v[:, g * 128:(g + 1) * 128]
        return acc

    def finish(h):
        count = total_of(lrecv, h, lsd, lrc)
        rank = 1.0 + (count - correction[:, h * half:(h + 1) * half])
        out_ref[:, h * half:(h + 1) * half] = jnp.log(rank)
        hit = 1.0 / (1.0 + jnp.exp(rank - 10.5))
        gain = hit * (0.6931471805599453 / jnp.log(1.0 + rank))
        return jnp.concatenate([lanes(hit), lanes(gain)], axis=0)

    zero = (jnp.zeros((8, 256), jnp.float32),) * tiles
    steps = n_rows // ROWS

    wcopy.wait()
    for c in copies:
        c.wait()
    pick(0, gt)
    forward(0)
    join(0)
    send_tscore(0)
    forward(1)
    pick(1, gh)
    hscore0 = own_scores(gh, 0)
    tscore0 = total_of(trecv, 0, tsd, trc)
    sums = score(0, tscore0, 0, steps // 2, zero)
    join(1)
    send_tscore(1)
    hscore1 = own_scores(gh, 1)
    sums = score(0, tscore0, steps // 2, steps, sums)
    send_count(0, sums, hscore0, tscore0)
    tscore1 = total_of(trecv, 1, tsd, trc)
    sums = score(1, tscore1, 0, steps, zero)
    send_count(1, sums, hscore1, tscore1)
    both = finish(0)
    both = both + finish(1)
    mval[...] = both
    for j in range(1, nu):
        pltpu.make_async_remote_copy(
            src_ref=mval, dst_ref=mrecv.at[mx], send_sem=msd, recv_sem=mrc,
            device_id={"users": lax.rem(mx + j, nu)}, device_id_type=MESH,
        ).start()
    mrecv[mx] = both
    wait_bytes(mrecv.at[pl.ds(0, nu - 1)], msd, mrc, "users")
    met = mrecv[0]
    for k in range(1, nu):
        met = met + mrecv[k]
    met_ref[...] = jnp.sum(met, axis=1, keepdims=True) * (1.0 / (users * nu))


def body(user_emb, item_emb, target, history):
    ni = lax.axis_size("items")
    nu = lax.axis_size("users")
    users = target.shape[0]
    n_rows, d = item_emb.shape
    half = users // HALVES
    vmem = pl.BlockSpec(memory_space=pltpu.VMEM)
    hbm = pl.BlockSpec(memory_space=pl.ANY)
    dma = pltpu.SemaphoreType.DMA
    ht = history.T
    lr, met = pl.pallas_call(
        functools.partial(kernel, ni, nu),
        out_shape=(jax.ShapeDtypeStruct((1, users), jnp.float32), jax.ShapeDtypeStruct((2, 1), jnp.float32)),
        in_specs=[vmem, vmem, vmem, hbm],
        out_specs=(vmem, vmem),
        scratch_shapes=[
            pltpu.VMEM((n_rows // 16, 16, d), jnp.bfloat16),
            pltpu.VMEM((HALVES, ni, d // ni, half), jnp.bfloat16),
            pltpu.VMEM((d, users), jnp.bfloat16),
            pltpu.VMEM((users, d), jnp.bfloat16),
            pltpu.VMEM((users, d), jnp.bfloat16),
            pltpu.VMEM((4, users // 128, 128), jnp.int32),
            pltpu.SMEM((4, users // 128, 128), jnp.int32),
            pltpu.VMEM((HALVES, 1, half), jnp.float32),
            pltpu.VMEM((HALVES, 1, half), jnp.float32),
            pltpu.VMEM((2, 128), jnp.float32),
            pltpu.VMEM((HALVES, ni, 1, half), jnp.float32),
            pltpu.VMEM((HALVES, ni, 1, half), jnp.float32),
            pltpu.VMEM((nu, 2, 128), jnp.float32),
            dma((PARTS,)), dma,
            dma((HALVES,)), dma((HALVES,)), dma((HALVES,)), dma((HALVES,)),
            dma((HALVES,)), dma((HALVES,)), dma((HALVES,)), dma((HALVES,)),
            dma, dma,
        ],
        compiler_params=pltpu.CompilerParams(
            collective_id=0, has_side_effects=True, vmem_limit_bytes=56 * 2**20
        ),
        name="rank_metrics",
    )(user_emb.T, target.reshape(1, users), ht, item_emb.reshape(n_rows // 16, 16, d))
    return lr.reshape(users), met.reshape(2)


def solution(mesh):
    return jax.shard_map(
        body,
        mesh=mesh,
        in_specs=(P("users", "items"), P("items", None), P("users"), P("users", None)),
        out_specs=(P("users"), P()),
        check_vma=False,
    )
```

time: 61.6 us -> 51.8 us (0.84)
  Pallas kernels: 58.2 us -> 48.4 us
    pallas_call x1, Pallas kernels: 58.2 us -> 48.4 us  [body(): pl.pallas_call(functools.partial(kernel, ni, nu), out_shape=(jax.ShapeDty...]
where the time goes in v2:
time: 51.8 us; the launch traced here: 51.6 us
  Pallas kernels  48.4 us (93%)
  other arithmetic  1.29 us (2%)
  local copies, waits for them, and re-layouts  1.27 us (2%)
  between operations  0.64 us (1%)
    pallas_call x1, Pallas kernels, body(): pl.pallas_call(functools.partial(kernel, ni, nu), out_shape=(jax.ShapeDty...  48.4 us
    pallas_call x1, other arithmetic, body(): pl.pallas_call(functools.partial(kernel, ni, nu), out_shape=(jax.ShapeDty...  1.29 us
    unnamed x1, local copies, waits for them, and re-layouts  1.27 us

profile of v2, /device:TPU:0, one launch (start us, length us, event | category | flops | bytes accessed | tf_op | source)
XLA Modules:
  0.0 51.6 jit_solution(11929788513650248184)
XLA Ops:
  0.6 48.4 %rank_metrics.1 = (f32[1,1024]{1,0:T(1,128)}, f32[2,1]{1,0:T(2,128)}) custom-call(bf16[8,1024]{1,0:T(8,128)(2,1)} %bitcast.7, s32[1,1024]{1,0:T(1,128)} %bitcast.9, s32[32,1024]{1,0:T(8,128)} %bitcast.6, bf16[2048,16,256]{2,1,0:T(8,128)(2,1)} %bitcast.5), custom_call_target="tpu_custom_call" | custom-call | tf_op jit(solution)/shard_map/rank_metrics/pallas_call | solution.py:239
  49.0 1.3 %reduce = f32[2]{0:T(128)} reduce(f32[2,1]{1,0:T(2,128)} %get-tuple-element.5, f32[]{:T(128)} %constant.1), dimensions={1}, to_apply=%get-tuple-element.5.reduce_sub_computation | reduce | bytes 20 | tf_op jit(solution)/shard_map/rank_metrics/pallas_call | solution.py:239
  50.3 1.3 %copy.7 = f32[1024]{0:T(1024)} copy(f32[1024]{0:T(1024)} %bitcast.8) | data formatting | bytes 8192

commit v3 on v2

--- a/solution.py
+++ b/solution.py
@@ -33,9 +33,10 @@
     d.wait_send()
 
 
-def kernel(ni, nu, u_ref, t_ref, h_ref, items_ref, out_ref, met_ref,
+def kernel(ni, nu, u_hbm, t_hbm, h_hbm, items_ref, out_ref, met_ref,
+           u_ref, t_ref, h_ref,
            buf, uall, U, gt, gh, where_v, where_s, tval, lval, mval, trecv, lrecv, mrecv,
-           isem, wsem, us, ur, ps, pr, tsd, trc, lsd, lrc, msd, mrc):
+           isem, wsem, asem, us, ur, ps, pr, tsd, trc, lsd, lrc, msd, mrc):
     n_tiles, sub, d = buf.shape
     n_rows = n_tiles * sub
     users = t_ref.shape[1]
@@ -65,6 +66,17 @@
                 device_id={"items": peer(s)}, device_id_type=MESH,
             ).start()
 
+    small = [
+        pltpu.make_async_copy(src, dst, asem.at[k])
+        for k, (src, dst) in enumerate(((u_hbm, u_ref), (t_hbm, t_ref), (h_hbm, h_ref)))
+    ]
+    for c in small:
+        c.start()
+    barrier = pltpu.get_barrier_semaphore()
+    for s in everyone:
+        pl.semaphore_signal(barrier, inc=1, device_id={"items": peer(s)}, device_id_type=MESH)
+    for j in range(1, nu):
+        pl.semaphore_signal(barrier, inc=1, device_id={"users": lax.rem(mx + j, nu)}, device_id_type=MESH)
     part = n_tiles // PARTS
     copies = [
         pltpu.make_async_copy(items_ref.at[pl.ds(p * part, part)], buf.at[pl.ds(p * part, part)], isem.at[p])
@@ -72,27 +84,24 @@
     ]
     for c in copies:
         c.start()
+    small[0].wait()
+    pl.semaphore_wait(barrier, ni + nu - 2)
+
+    for h in range(HALVES):
+        to_all(u_ref.at[:, pl.ds(h * half, half)], uall.at[h, me], us.at[h], ur.at[h], same_core)
+    for c in small[1:]:
+        c.wait()
     for k, ids in enumerate((t_ref[...], h_ref[pl.ds(me, 1), :])):
         slab, row = lax.shift_right_logical(ids, 4) & (n_tiles - 1), ids & (sub - 1)
         for g in range(users // 128):
             where_v[2 * k, g:g + 1, :] = slab[:, g * 128:(g + 1) * 128]
             where_v[2 * k + 1, g:g + 1, :] = row[:, g * 128:(g + 1) * 128]
-    wcopy = pltpu.make_async_copy(where_v, where_s, wsem)
-
-    barrier = pltpu.get_barrier_semaphore()
-    for s in everyone:
-        pl.semaphore_signal(barrier, inc=1, device_id={"items": peer(s)}, device_id_type=MESH)
-    for j in range(1, nu):
-        pl.semaphore_signal(barrier, inc=1, device_id={"users": lax.rem(mx + j, nu)}, device_id_type=MESH)
-    wcopy.start()
     seen = jnp.max(jnp.where(h_ref[...] == t_ref[...], 1.0, 0.0), axis=0, keepdims=True)
     correction = 0.5 - 0.5 * seen
-    pl.semaphore_wait(barrier, ni + nu - 2)
-
-    for h in range(HALVES):
-        to_all(u_ref.at[:, pl.ds(h * half, half)], uall.at[h, me], us.at[h], ur.at[h], same_core)
     for h in range(HALVES):
         uall[h, me] = u_ref[:, h * half:(h + 1) * half]
+    wcopy = pltpu.make_async_copy(where_v, where_s, wsem)
+    wcopy.start()
 
     row16 = lax.broadcasted_iota(jnp.int32, (16, 128), 0)
     lane16 = lax.broadcasted_iota(jnp.int32, (16, 256), 1) - 16 * lax.broadcasted_iota(jnp.int32, (16, 256), 0)
@@ -223,7 +232,13 @@
     met = mrecv[0]
     for k in range(1, nu):
         met = met + mrecv[k]
-    met_ref[...] = jnp.sum(met, axis=1, keepdims=True) * (1.0 / (users * nu))
+    met_ref[...] = met
+
+
+def hand_over(lr_ref, met_ref, lr_out, met_out, *, scale):
+    lr_out[...] = lr_ref[...]
+    v = jnp.sum(met_ref[...], axis=1, keepdims=True) * scale
+    met_out[...] = jnp.concatenate([v[0:1], v[1:2]], axis=1)
 
 
 def body(user_emb, item_emb, target, history):
@@ -238,10 +253,13 @@
     ht = history.T
     lr, met = pl.pallas_call(
         functools.partial(kernel, ni, nu),
-        out_shape=(jax.ShapeDtypeStruct((1, users), jnp.float32), jax.ShapeDtypeStruct((2, 1), jnp.float32)),
-        in_specs=[vmem, vmem, vmem, hbm],
+        out_shape=(pltpu.VMEM((1, users), jnp.float32), pltpu.VMEM((2, 128), jnp.float32)),
+        in_specs=[hbm, hbm, hbm, hbm],
         out_specs=(vmem, vmem),
         scratch_shapes=[
+            pltpu.VMEM((d // ni, users), jnp.bfloat16),
+            pltpu.VMEM((1, users), jnp.int32),
+            pltpu.VMEM((ni, users), jnp.int32),
             pltpu.VMEM((n_rows // 16, 16, d), jnp.bfloat16),
             pltpu.VMEM((HALVES, ni, d // ni, half), jnp.bfloat16),
             pltpu.VMEM((d, users), jnp.bfloat16),
@@ -255,7 +273,7 @@
             pltpu.VMEM((HALVES, ni, 1, half), jnp.float32),
             pltpu.VMEM((HALVES, ni, 1, half), jnp.float32),
             pltpu.VMEM((nu, 2, 128), jnp.float32),
-            dma((PARTS,)), dma,
+            dma((PARTS,)), dma, dma((3,)),
             dma((HALVES,)), dma((HALVES,)), dma((HALVES,)), dma((HALVES,)),
             dma((HALVES,)), dma((HALVES,)), dma((HALVES,)), dma((HALVES,)),
             dma, dma,
@@ -265,6 +283,13 @@
         ),
         name="rank_metrics",
     )(user_emb.T, target.reshape(1, users), ht, item_emb.reshape(n_rows // 16, 16, d))
+    lr, met = pl.pallas_call(
+        functools.partial(hand_over, scale=1.0 / (users * nu)),
+        out_shape=(jax.ShapeDtypeStruct((1, users), jnp.float32), jax.ShapeDtypeStruct((1, 2), jnp.float32)),
+        in_specs=[vmem, vmem],
+        out_specs=(vmem, vmem),
+        name="hand_over",
+    )(*(pltpu.with_memory_space_constraint(v, pltpu.VMEM) for v in (lr, met)))
     return lr.reshape(users), met.reshape(2)
 
 

time: 51.8 us -> 48.6 us (0.938)
  other arithmetic: 1.29 us -> 0 us
  local copies, waits for them, and re-layouts: 1.27 us -> 0 us
  Pallas kernels: 48.4 us -> 47.7 us
    pallas_call x1 -> x0, other arithmetic: 1.29 us -> none  [body(): pl.pallas_call(functools.partial(kernel, ni, nu), out_shape=(jax.ShapeDty...]
    unnamed x1 -> x0, local copies, waits for them, and re-layouts: 1.27 us -> none
    pallas_call x1 -> x2, Pallas kernels: 48.4 us -> 47.7 us  [the longest x1 47.1 us: body(): pl.pallas_call(functools.partial(kernel, ni, nu), out_shape=(pltpu.VMEM((...]
where the time goes in v3:
time: 48.6 us; the launch traced here: 48.4 us
  Pallas kernels  47.7 us (98%)
  between operations  0.64 us (1%)
    pallas_call x1, Pallas kernels, body(): pl.pallas_call(functools.partial(kernel, ni, nu), out_shape=(pltpu.VMEM((...  47.1 us

profile of v3, /device:TPU:0, one launch (start us, length us, event | category | flops | bytes accessed | tf_op | source)
XLA Modules:
  0.0 48.4 jit_solution(11720199356879875791)
XLA Ops:
  0.6 47.1 %rank_metrics.1 = (f32[1,1024]{1,0:T(1,128)S(1)}, f32[2,128]{1,0:T(2,128)S(1)}) custom-call(bf16[8,1024]{1,0:T(8,128)(2,1)} %bitcast.8, s32[1,1024]{1,0:T(1,128)} %bitcast.9, s32[32,1024]{1,0:T(8,128)} %bitcast.7, bf16[2048,16,256]{2,1,0:T(8,128)(2,1)} %bitcast.6), custom_call_target="tpu_custom_call" | custom-call | tf_op jit(solution)/shard_map/rank_metrics/pallas_call | solution.py:254
  47.8 0.6 %hand_over.1 = (f32[1,1024]{1,0:T(1,128)}, f32[1,2]{1,0:T(1,128)}) custom-call(f32[1,1024]{1,0:T(1,128)S(1)} %get-tuple-element.6.lr_ref, f32[2,128]{1,0:T(2,128)S(1)} %get-tuple-element.7.met_ref), custom_call_target="tpu_custom_call" | custom-call | tf_op jit(solution)/shard_map/hand_over/pallas_call | solution.py:286

commit v4 on v3

--- a/solution.py
+++ b/solution.py
@@ -9,7 +9,7 @@
 
 MESH = pl.DeviceIdType.MESH
 SHARP_HALF = 2.0
-ROWS = 8192
+ROWS = 16384
 PARTS = 8
 
 
@@ -208,13 +208,12 @@
     send_tscore(0)
     forward(1)
     pick(1, gh)
-    hscore0 = own_scores(gh, 0)
-    tscore0 = total_of(trecv, 0, tsd, trc)
-    sums = score(0, tscore0, 0, steps // 2, zero)
     join(1)
     send_tscore(1)
+    hscore0 = own_scores(gh, 0)
     hscore1 = own_scores(gh, 1)
-    sums = score(0, tscore0, steps // 2, steps, sums)
+    tscore0 = total_of(trecv, 0, tsd, trc)
+    sums = score(0, tscore0, 0, steps, zero)
     send_count(0, sums, hscore0, tscore0)
     tscore1 = total_of(trecv, 1, tsd, trc)
     sums = score(1, tscore1, 0, steps, zero)

time: 48.6 us -> 47.1 us (0.969)
  Pallas kernels: 47.7 us -> 46.3 us
    pallas_call x1, Pallas kernels: 47.1 us -> 45.7 us  [body(): pl.pallas_call(functools.partial(kernel, ni, nu), out_shape=(pltpu.VMEM((...]
where the time goes in v4:
time: 47.1 us; the launch traced here: 47 us
  Pallas kernels  46.3 us (98%)
  between operations  0.64 us (1%)
    pallas_call x1, Pallas kernels, body(): pl.pallas_call(functools.partial(kernel, ni, nu), out_shape=(pltpu.VMEM((...  45.7 us

profile of v4, /device:TPU:0, one launch (start us, length us, event | category | flops | bytes accessed | tf_op | source)
XLA Modules:
  0.0 47.0 jit_solution(6406860570927254431)
XLA Ops:
  0.6 45.7 %rank_metrics.1 = (f32[1,1024]{1,0:T(1,128)S(1)}, f32[2,128]{1,0:T(2,128)S(1)}) custom-call(bf16[8,1024]{1,0:T(8,128)(2,1)} %bitcast.8, s32[1,1024]{1,0:T(1,128)} %bitcast.9, s32[32,1024]{1,0:T(8,128)} %bitcast.7, bf16[2048,16,256]{2,1,0:T(8,128)(2,1)} %bitcast.6), custom_call_target="tpu_custom_call" | custom-call | tf_op jit(solution)/shard_map/rank_metrics/pallas_call | solution.py:253
  46.4 0.6 %hand_over.1 = (f32[1,1024]{1,0:T(1,128)}, f32[1,2]{1,0:T(1,128)}) custom-call(f32[1,1024]{1,0:T(1,128)S(1)} %get-tuple-element.6.lr_ref, f32[2,128]{1,0:T(2,128)S(1)} %get-tuple-element.7.met_ref), custom_call_target="tpu_custom_call" | custom-call | tf_op jit(solution)/shard_map/hand_over/pallas_call | solution.py:285

commit v5 on v4

--- a/solution.py
+++ b/solution.py
@@ -10,7 +10,7 @@
 MESH = pl.DeviceIdType.MESH
 SHARP_HALF = 2.0
 ROWS = 16384
-PARTS = 8
+PARTS = 4
 
 
 HALVES = 2

time: 47.1 us -> 47.1 us (level)
  no operation moved by 1% of the time
where the time goes in v5:
time: 47.1 us; the launch traced here: 47 us
  Pallas kernels  46.3 us (98%)
  between operations  0.64 us (1%)
    pallas_call x1, Pallas kernels, body(): pl.pallas_call(functools.partial(kernel, ni, nu), out_shape=(pltpu.VMEM((...  45.7 us

profile of v5, /device:TPU:0, one launch (start us, length us, event | category | flops | bytes accessed | tf_op | source)
XLA Modules:
  0.0 47.0 jit_solution(6024766163658773570)
XLA Ops:
  0.6 45.7 %rank_metrics.1 = (f32[1,1024]{1,0:T(1,128)S(1)}, f32[2,128]{1,0:T(2,128)S(1)}) custom-call(bf16[8,1024]{1,0:T(8,128)(2,1)} %bitcast.8, s32[1,1024]{1,0:T(1,128)} %bitcast.9, s32[32,1024]{1,0:T(8,128)} %bitcast.7, bf16[2048,16,256]{2,1,0:T(8,128)(2,1)} %bitcast.6), custom_call_target="tpu_custom_call" | custom-call | tf_op jit(solution)/shard_map/rank_metrics/pallas_call | solution.py:253
  46.4 0.6 %hand_over.1 = (f32[1,1024]{1,0:T(1,128)}, f32[1,2]{1,0:T(1,128)}) custom-call(f32[1,1024]{1,0:T(1,128)S(1)} %get-tuple-element.6.lr_ref, f32[2,128]{1,0:T(2,128)S(1)} %get-tuple-element.7.met_ref), custom_call_target="tpu_custom_call" | custom-call | tf_op jit(solution)/shard_map/hand_over/pallas_call | solution.py:285
